TPU v7x, 32 devices: a whole 2x2x4 slice. The times are simulated.
32 devices in a mesh: rep: 2 (over y), span: 2 (over core), seq: 4 (over z), tp: 2 (over x).
Axes of the slice: x: 2, y: 2, z: 4, core: 2. Of those that a mesh axis runs over, the one named last changes fastest.
Arguments:
- queries: bfloat16 [8, 512, 24, 128], P(('rep', 'span'), 'seq', 'tp'), parts along dimension 0, may hold values from -110 to 110
- key_states: bfloat16 [8, 512, 4, 128], P(('rep', 'span'), 'seq', 'tp'), parts along dimension 0, may hold values from -11 to 11
- value_states: bfloat16 [8, 512, 4, 128], P(('rep', 'span'), 'seq', 'tp'), parts along dimension 0, may hold values from -6 to 6
- out_weight: bfloat16 [3072, 6144], P('tp', 'seq'), may hold values from -0.109375 to 0.109375
- noise_table: float32 [64, 6144], P(None, 'tp'), may hold values from 0.5 to 2
- plan: int32 [8], P('rep'), parts along dimension 0, may hold values from 0 to 63
Outputs:
- branch_out: bfloat16 [8, 512, 6144], P(('rep', 'span'), 'seq', 'tp'), parts along dimension 0
There are 2 independent parts, one for each index of `rep`. A program takes and returns all parts, laid end to end along the dimension named above; an argument that names none is the same for every part. Nothing has to cross between parts.
All inputs are finite; a program needn't handle non-finite values.
Results may differ from a plain program's by a relative error of at most 0.014.
Values may be sent and summed in bfloat16 or wider, within the bound.
A program may use at most 128 MiB of HBM per device.

v0:
```python
import jax
import jax.numpy as jnp
from jax import lax
from jax.sharding import PartitionSpec as P


def fold_block(carried, query_rows, key_rows, value_rows, factor):
    maxima, totals, weighted = carried
    scores = (
        jnp.einsum("tkgd,skd->tkgs", query_rows, key_rows, preferred_element_type=jnp.float32)
        * factor
    )
    highest = jnp.maximum(maxima, jnp.max(scores, axis=-1))
    shrink = jnp.exp(maxima - highest)
    weights = jnp.exp(scores - highest[..., None])
    totals = totals * shrink + jnp.sum(weights, axis=-1)
    weighted = weighted * shrink[..., None] + jnp.einsum(
        "tkgs,skd->tkgd",
        weights.astype(jnp.bfloat16),
        value_rows,
        preferred_element_type=jnp.float32,
    )
    return (maxima * 0.0 + highest, totals, weighted)


def per_device(queries, key_states, value_states, out_weight, noise_table, plan):
    ch_dev, tok_dev, heads_local, head_size = queries.shape
    kv_local = key_states.shape[2]
    per_kv = heads_local // kv_local
    span_count = ch_dev * lax.axis_size("span")
    first_span = lax.axis_index("span") * ch_dev
    factor = head_size ** (-0.5)
    grouped = queries.reshape(ch_dev, tok_dev, kv_local, per_kv, head_size)
    start_max = jnp.full((ch_dev, tok_dev, kv_local, per_kv), -1e30, jnp.float32)
    start_tot = jnp.zeros((ch_dev, tok_dev, kv_local, per_kv), jnp.float32)
    start_acc = jnp.zeros((ch_dev, tok_dev, kv_local, per_kv, head_size), jnp.float32)
    span_rows = (
        lax.all_gather(key_states, "seq", axis=1, tiled=True),
        lax.all_gather(value_states, "seq", axis=1, tiled=True),
    )
    key_piece = lax.all_gather(span_rows[0], "span", axis=0, tiled=True)
    value_piece = lax.all_gather(span_rows[1], "span", axis=0, tiled=True)
    new_max = []
    new_tot = []
    new_acc = []
    for q_span in range(ch_dev):
        inner_state = (start_max[q_span], start_tot[q_span], start_acc[q_span])
        for k_span in range(span_count):

            def update(inner, q_span=q_span, k_span=k_span):
                return fold_block(
                    inner, grouped[q_span], key_piece[k_span], value_piece[k_span], factor
                )

            inner_state = lax.cond(
                k_span <= first_span + q_span, update, lambda inner: inner, inner_state
            )
        new_max.append(inner_state[0])
        new_tot.append(inner_state[1])
        new_acc.append(inner_state[2])
    attn = (
        (jnp.stack(new_acc) / jnp.stack(new_tot)[..., None])
        .reshape(ch_dev, tok_dev, heads_local * head_size)
        .astype(jnp.bfloat16)
    )
    columns = jnp.einsum(
        "ctf,fo->cto",
        lax.all_gather(attn, "seq", axis=1, tiled=True),
        out_weight,
        preferred_element_type=jnp.float32,
    )
    partial_out = lax.all_to_all(
        columns.astype(jnp.bfloat16), "seq", split_axis=1, concat_axis=2, tiled=True
    ).astype(columns.dtype)
    summed = lax.psum_scatter(
        partial_out.astype(jnp.bfloat16), "tp", scatter_dimension=2, tiled=True
    ).astype(jnp.float32)
    levels = lax.dynamic_slice_in_dim(plan, first_span, ch_dev)
    picks = (levels[:, None] == jnp.arange(noise_table.shape[0], dtype=jnp.int32)[None, :]).astype(
        jnp.float32
    )
    gates = jnp.dot(picks, noise_table, precision=lax.Precision.HIGHEST)
    return (summed * gates[:, None, :]).astype(jnp.bfloat16)


def solution(mesh):
    placed = (
        P(("rep", "span"), "seq", "tp", None),
        P(("rep", "span"), "seq", "tp", None),
        P(("rep", "span"), "seq", "tp", None),
        P("tp", "seq"),
        P(None, "tp"),
        P("rep"),
    )
    return jax.shard_map(
        per_device,
        mesh=mesh,
        in_specs=placed,
        out_specs=P(("rep", "span"), "seq", "tp"),
        check_vma=False,
    )
```

profile of v0, /device:TPU:0, one launch (start us, length us, event | category | flops | bytes accessed | tf_op | source)
XLA Modules:
  0.0 320.5 jit_solution(18199733619609409647)
XLA Ops:
  6.5 1.0 copy.63
  7.5 18.0 %all_gather.15 = bf16[2,512,2,128]{3,1,2,0:T(8,128)(2,1)} all-gather(bf16[2,128,2,128]{3,1,2,0:T(8,128)(2,1)S(1)} %copy.63), channel_id=1, replica_groups=mesh['rep'=2,'span'=2,'seq'=4,'tp'=2] {'seq'}, dimensions={1}, use_global_device_ids=true | all-gather | bytes 655360 | tf_op jit(solution)/shard_map/all_gather | solution.py:38
  25.6 0.0 all-gather.6.cloned.1.call-start
  25.6 0.9 copy.64
  26.5 17.0 %all_gather.17 = bf16[2,512,2,128]{3,1,2,0:T(8,128)(2,1)} all-gather(bf16[2,128,2,128]{3,1,2,0:T(8,128)(2,1)S(1)} %copy.64), channel_id=1, replica_groups=mesh['rep'=2,'span'=2,'seq'=4,'tp'=2] {'seq'}, dimensions={1}, use_global_device_ids=true | all-gather | bytes 655360 | tf_op jit(solution)/shard_map/all_gather | solution.py:39
  43.6 0.0 all-gather.8.cloned.1.call-start
  43.7 9.6 %all-gather.6.cloned.1.call-done = bf16[4,512,2,128]{3,1,2,0:T(8,128)(2,1)} async-done(((bf16[2,512,2,128]{3,1,2,0:T(8,128)(2,1)}), bf16[4,512,2,128]{3,1,2,0:T(8,128)(2,1)}) %all-gather.6.cloned.1.call-update) | async-done | bytes 1048592 | tf_op jit(solution)/shard_map/all_gather | solution.py:42
  53.3 6.1 %conditional.12 = (f32[128,2,6]{0,2,1:T(8,128)}, f32[128,2,6]{0,2,1:T(8,128)S(1)}, f32[128,2,6,128]{3,0,2,1:T(8,128)S(1)}) conditional(s32[]{:T(128)} %convert_element_type.70, () %tuple.93, (bf16[4,512,2,128]{3,1,2,0:T(8,128)(2,1)}, bf16[2,128,2,6,128]{4,1,3,2,0:T(8,128)(2,1)}, bf16[4,512,2,128]{3,1,2,0:T(8,128)(2,1)}) %tuple.190), branch_computations={%region_16.0_spmd, %region_17.0_spmd} | conditional | flops 409147392 | bytes 11210776 | solution.py:55
  53.3 1.7 bitcast_reduce_fusion.4
  55.0 0.6 exponential_multiply_fusion.1
  55.6 1.2 fusion.85
  56.8 0.7 fusion.104
  57.5 1.9 fusion.93
  59.4 6.2 %conditional.13 = ((f32[128,2,6]{0,2,1:T(8,128)}, f32[128,2,6]{0,2,1:T(8,128)S(1)}, f32[128,2,6,128]{3,0,2,1:T(8,128)S(1)})) conditional(s32[]{:T(128)} %convert_element_type.69, (f32[128,2,6]{0,2,1:T(8,128)}, f32[128,2,6]{0,2,1:T(8,128)S(1)}, f32[128,2,6,128]{3,0,2,1:T(8,128)S(1)}) %conditional.12, (f32[128,2,6]{0,2,1:T(8,128)}, ...), branch_computations={%region_20.0_spmd, %region_21.0_spmd} | conditional | flops 409344000 | bytes 12032032 | solution.py:55
  59.4 1.7 bitcast_reduce_fusion.5
  61.1 0.7 multiply_add_fusion.5
  61.8 0.5 fusion.107
  62.3 0.7 multiply_add_fusion.4
  63.0 0.6 copy.113
  63.6 2.0 fusion.115
  65.6 6.1 %conditional.8 = (f32[128,2,6]{0,2,1:T(8,128)}, f32[128,2,6]{0,2,1:T(8,128)S(1)}, f32[128,2,6,128]{3,0,2,1:T(8,128)S(1)}) conditional(s32[]{:T(128)} %convert_element_type.66, () %tuple.87, (bf16[4,512,2,128]{3,1,2,0:T(8,128)(2,1)}, bf16[2,128,2,6,128]{4,1,3,2,0:T(8,128)(2,1)}, bf16[4,512,2,128]{3,1,2,0:T(8,128)(2,1)}) %tuple.193), branch_computations={%region_0.0_spmd, %region_1.0_spmd} | conditional | flops 409147392 | bytes 11210776 | solution.py:55
  65.6 1.7 bitcast_reduce_fusion
  67.3 0.6 exponential_multiply_fusion
  67.9 1.2 fusion.2
  69.1 0.7 fusion.21
  69.8 1.9 fusion.10
  71.8 0.2 conditional.10
  72.0 1.5 conditional.15
  72.0 0.3 copy.68
  72.2 1.2 copy.102
  73.4 1.4 conditional.11
  73.4 0.3 copy.65
  73.7 1.2 copy.100
  74.9 0.1 div.11
  75.0 1.6 copy.73
  76.6 2.9 fusion.171
  79.6 0.0 reduce-scatter.2.cloned.1.call-start
  79.6 93.0 %all-gather.8.cloned.1.call-done = bf16[2,512,1536]{2,1,0:T(8,128)(2,1)} async-done(((bf16[2,128,1536]{2,1,0:T(8,128)(2,1)}), bf16[2,512,1536]{2,1,0:T(8,128)(2,1)}) %all-gather.8.cloned.1.call-update) | async-done | bytes 3145744 | tf_op jit(solution)/shard_map/all_gather | solution.py:68
  172.6 8.1 %fusion.168 = bf16[2,512,1536]{2,1,0:T(8,128)(2,1)S(1)} fusion(bf16[2,512,1536]{2,1,0:T(8,128)(2,1)} %all-gather.8.cloned.1.call-done, bf16[1536,1536]{1,0:T(8,128)(2,1)} %param.25), kind=kOutput, calls=%fused_computation.166 | convolution fusion | flops 4833411072 | bytes 11010048 | tf_op jit(solution)/shard_map/ctf,fo->cto/dot_general | solution.py:66
  180.7 3.2 %copy.74 = bf16[2,512,1536]{2,0,1:T(2,128)(2,1)S(1)} copy(bf16[2,512,1536]{2,1,0:T(8,128)(2,1)S(1)} %fusion.168) | data formatting | bytes 6291456 | tf_op jit(solution)/shard_map/convert_element_type | solution.py:73
  183.9 73.3 %all_to_all.18 = bf16[2,512,1536]{2,0,1:T(2,128)(2,1)S(1)} all-to-all(bf16[2,512,1536]{2,0,1:T(2,128)(2,1)S(1)} %copy.74), channel_id=1, replica_groups=mesh['rep'=2,'span'=2,'seq'=4,'tp'=2] {'seq'}, dimensions={1} | all-to-all | bytes 6291456 | tf_op jit(solution)/shard_map/all_to_all | solution.py:72
  257.2 4.1 %copy.75 = bf16[2,128,4,1536]{3,2,1,0:T(4,128)(2,1)} copy(bf16[2,128,4,1536]{3,0,1,2:T(2,128)(2,1)S(1)} %bitcast.326) | data formatting | bytes 6291456 | tf_op jit(solution)/shard_map/all_to_all | solution.py:72
  261.3 6.9 %all_to_all.16 = bf16[2,128,6144]{2,1,0:T(8,128)(2,1)} reshape(bf16[2,128,4,1536]{3,2,1,0:T(4,128)(2,1)} %copy.75) | data formatting | bytes 6291456 | tf_op jit(solution)/shard_map/all_to_all | solution.py:72
  268.3 0.6 copy-done.5
  268.9 0.1 dynamic_slice.3
  269.0 0.4 fusion.172
  269.4 41.7 %reduce-scatter.2.cloned.1.call-done = bf16[2,128,3072]{2,1,0:T(8,128)(2,1)} async-done(((bf16[2,128,6144]{2,1,0:T(8,128)(2,1)}), bf16[2,128,3072]{2,1,0:T(8,128)(2,1)}) %reduce-scatter.2.cloned.1.call-update) | async-done | bytes 1572880 | tf_op jit(solution)/shard_map/reduce_scatter | solution.py:75
  311.1 2.9 multiply_convert_fusion
  (12 shorter events, 0.1 us)
Async XLA Ops:
  6.5 262.4 %copy-start = (f32[64,3072]{1,0:T(8,128)S(1)}, f32[64,3072]{1,0:T(8,128)}, u32[]{:S(2)}) copy-start(f32[64,3072]{1,0:T(8,128)} %param.26) | copy-start | bytes 2359300
  6.5 37.2 %all-gather.4.cloned.1.call-start = ((), (), s32[]{:S(2)}) async-start(), calls=%async_computation.2 | async-start | bytes 1572864 | tf_op jit(solution)/shard_map/all_gather | solution.py:41
  25.6 27.7 %all-gather.6.cloned.1.call-start = ((), (), s32[]{:S(2)}) async-start(), calls=%async_computation.3 | async-start | bytes 1572864 | tf_op jit(solution)/shard_map/all_gather | solution.py:42
  43.6 129.0 %all-gather.8.cloned.1.call-start = ((), (), s32[]{:S(2)}) async-start(), calls=%async_computation.4 | async-start | bytes 3932160 | tf_op jit(solution)/shard_map/all_gather | solution.py:68
  79.6 231.5 %reduce-scatter.2.cloned.1.call-start = ((), (), s32[]{:S(2)}) async-start(), calls=%async_computation.5 | async-start | bytes 4718592 | tf_op jit(solution)/shard_map/reduce_scatter | solution.py:75
  268.3 0.7 copy-start.5
Sparse Core Ops, SparseCore 0:
  25.7 10.8 all-gather.3
  43.7 9.5 all-gather.5
  79.7 92.8 all-gather.7
  268.4 42.6 reduce-scatter.1
where the time goes:
time: 322 us; the launch traced here: 321 us
  waiting for transfers between devices  144 us (45%)
  blocking collectives  108 us (34%)
  local copies, waits for them, and re-layouts  22.1 us (7%)
  matrix products  19.2 us (6%)
  between operations  13.2 us (4%)
  other arithmetic  12.9 us (4%)
    all_gather x1, waiting for transfers between devices, per_device(): lax.all_gather(attn, 'seq', axis=1, tiled=True)  93 us
    all_to_all x1, blocking collectives, per_device(): lax.all_to_all(columns.astype(jnp.bfloat16), 'seq', split_axis=1, concat_...  73.3 us
    reduce_scatter x1, waiting for transfers between devices, per_device(): lax.psum_scatter(partial_out.astype(jnp.bfloat16), 'tp', scatter_dimensio...  41.7 us
    all_gather x1, blocking collectives, per_device(): lax.all_gather(key_states, 'seq', axis=1, tiled=True)  18 us
    all_gather x1, blocking collectives, per_device(): lax.all_gather(value_states, 'seq', axis=1, tiled=True)  17 us
    all_to_all x2, local copies, waits for them, and re-layouts, per_device(): lax.all_to_all(columns.astype(jnp.bfloat16), 'seq', split_axis=1, concat_...  11 us
    all_gather x1, waiting for transfers between devices, per_device(): value_piece = lax.all_gather(span_rows[1], 'span', axis=0, tiled=True)  9.6 us
    dot_general x1, matrix products, per_device(): jnp.einsum('ctf,fo->cto', lax.all_gather(attn, 'seq', axis=1, tiled=True)...  8.06 us
  transfers between devices with their start and end apart: 4, of which 3 were waited for; matrix products, arithmetic and copies ran while one was open for 0% of the time, Pallas kernels for 0%

commit v1 on v0

--- a/solution.py
+++ b/solution.py
@@ -2,6 +2,32 @@
 import jax.numpy as jnp
 from jax import lax
 from jax.sharding import PartitionSpec as P
+
+
+def on_each_block(x, axis, dim, work, out_dim):
+    devices, index, width = (lax.axis_size(axis), lax.axis_index(axis), x.shape[dim])
+    right = [(i, (i + 1) % devices) for i in range(devices)]
+    downward = [(b, a) for a, b in right]
+    lower, upper = (lax.ppermute(x, axis, right), lax.ppermute(x, axis, downward))
+    made = work(x, index * width)
+    length = made.shape[out_dim]
+    filled = jnp.zeros(
+        (*made.shape[:out_dim], devices * length, *made.shape[out_dim + 1 :]), made.dtype
+    )
+
+    def put(filled, made, owner):
+        return lax.dynamic_update_slice_in_dim(filled, made, owner * length, axis=out_dim)
+
+    filled = put(filled, made, index)
+    for step in range(1, devices // 2 + 1):
+        below, above = ((index - step) % devices, (index + step) % devices)
+        held = (lower, upper)
+        if step < devices // 2:
+            lower, upper = (lax.ppermute(lower, axis, right), lax.ppermute(upper, axis, downward))
+        filled = put(filled, work(held[0], below * width), below)
+        if 2 * step < devices:
+            filled = put(filled, work(held[1], above * width), above)
+    return filled
 
 
 def fold_block(carried, query_rows, key_rows, value_rows, factor):
@@ -63,11 +89,14 @@
         .reshape(ch_dev, tok_dev, heads_local * head_size)
         .astype(jnp.bfloat16)
     )
-    columns = jnp.einsum(
-        "ctf,fo->cto",
-        lax.all_gather(attn, "seq", axis=1, tiled=True),
-        out_weight,
-        preferred_element_type=jnp.float32,
+    columns = on_each_block(
+        attn,
+        "seq",
+        1,
+        lambda shard, at: jnp.einsum(
+            "ctf,fo->cto", shard, out_weight, preferred_element_type=jnp.float32
+        ),
+        1,
     )
     partial_out = lax.all_to_all(
         columns.astype(jnp.bfloat16), "seq", split_axis=1, concat_axis=2, tiled=True

time: 322 us -> 264 us (0.82)
  waiting for transfers between devices: 144 us -> 101 us
  blocking collectives: 108 us -> 93.1 us
  starting transfers between devices: 0.13 us -> 3.96 us
    all_gather x1 -> x0, waiting for transfers between devices: 93 us -> none  [per_device(): lax.all_gather(attn, 'seq', axis=1, tiled=True)]
    reduce_scatter x1, waiting for transfers between devices: 41.7 us -> 75.5 us  [per_device(): lax.psum_scatter(partial_out.astype(jnp.bfloat16), 'tp', scatter_dimensio...]
    ppermute x0 -> x3, waiting for transfers between devices: none -> 16 us  [the longest x1 6.23 us: on_each_block(): lax.ppermute(lower, axis, right)]
    all_to_all x1, blocking collectives: 73.3 us -> 58.1 us  [per_device(): lax.all_to_all(columns.astype(jnp.bfloat16), 'seq', split_axis=1, concat_...]
    all_to_all x2, local copies, waits for them, and re-layouts: 11 us -> 6.8 us  [per_device(): lax.all_to_all(columns.astype(jnp.bfloat16), 'seq', split_axis=1, concat_...]
    ppermute x0 -> x3, starting transfers between devices: none -> 3.88 us  [the longest x1 2.07 us: on_each_block(): lax.ppermute(x, axis, downward)]
    dynamic_update_slice x0 -> x4, local copies, waits for them, and re-layouts: none -> 3.55 us  [put(): lax.dynamic_update_slice_in_dim(filled, made, owner * length, axis=out_dim)]
    dot_general x1 -> x4, matrix products: 8.06 us -> 7.84 us  [per_device(): jnp.einsum('ctf,fo->cto', shard, out_weight, preferred_element_type=jnp.f...]
  transfers between devices with their start and end apart: 4 -> 6, of which waited for: 3 -> 5; matrix products, arithmetic and copies ran while one was open for 0% -> 5% of each run, Pallas kernels for 0% -> 0%
where the time goes in v1:
time: 264 us; the launch traced here: 263 us
  waiting for transfers between devices  101 us (38%)
  blocking collectives  93.1 us (35%)
  local copies, waits for them, and re-layouts  21.4 us (8%)
  matrix products  19 us (7%)
  between operations  13.3 us (5%)
  other arithmetic  11.1 us (4%)
  starting transfers between devices  3.96 us (2%)
    reduce_scatter x1, waiting for transfers between devices, per_device(): lax.psum_scatter(partial_out.astype(jnp.bfloat16), 'tp', scatter_dimensio...  75.5 us
    all_to_all x1, blocking collectives, per_device(): lax.all_to_all(columns.astype(jnp.bfloat16), 'seq', split_axis=1, concat_...  58.1 us
    all_gather x1, blocking collectives, per_device(): lax.all_gather(key_states, 'seq', axis=1, tiled=True)  18 us
    all_gather x1, blocking collectives, per_device(): lax.all_gather(value_states, 'seq', axis=1, tiled=True)  17 us
    all_gather x1, waiting for transfers between devices, per_device(): value_piece = lax.all_gather(span_rows[1], 'span', axis=0, tiled=True)  9.54 us
    dot_general x4, matrix products, per_device(): jnp.einsum('ctf,fo->cto', shard, out_weight, preferred_element_type=jnp.f...  7.84 us
    all_to_all x2, local copies, waits for them, and re-layouts, per_device(): lax.all_to_all(columns.astype(jnp.bfloat16), 'seq', split_axis=1, concat_...  6.8 us
    ppermute x1, waiting for transfers between devices, on_each_block(): lax.ppermute(lower, axis, right)  6.23 us
  transfers between devices with their start and end apart: 6, of which 5 were waited for; matrix products, arithmetic and copies ran while one was open for 5% of the time, Pallas kernels for 0%

profile of v1, /device:TPU:0, one launch (start us, length us, event | category | flops | bytes accessed | tf_op | source)
XLA Modules:
  0.0 263.1 jit_solution(16729916723101127039)
XLA Ops:
  6.5 1.0 copy.86
  7.5 18.0 %all_gather.12 = bf16[2,512,2,128]{3,1,2,0:T(8,128)(2,1)} all-gather(bf16[2,128,2,128]{3,1,2,0:T(8,128)(2,1)S(1)} %copy.86), channel_id=1, replica_groups=mesh['rep'=2,'span'=2,'seq'=4,'tp'=2] {'seq'}, dimensions={1}, use_global_device_ids=true | all-gather | bytes 655360 | tf_op jit(solution)/shard_map/all_gather | solution.py:64
  25.6 0.9 copy.87
  26.5 17.0 %all_gather.14 = bf16[2,512,2,128]{3,1,2,0:T(8,128)(2,1)} all-gather(bf16[2,128,2,128]{3,1,2,0:T(8,128)(2,1)S(1)} %copy.87), channel_id=1, replica_groups=mesh['rep'=2,'span'=2,'seq'=4,'tp'=2] {'seq'}, dimensions={1}, use_global_device_ids=true | all-gather | bytes 655360 | tf_op jit(solution)/shard_map/all_gather | solution.py:65
  43.8 9.5 %all-gather.5.cloned.1.call-done = bf16[4,512,2,128]{3,1,2,0:T(8,128)(2,1)} async-done(((bf16[2,512,2,128]{3,1,2,0:T(8,128)(2,1)}), bf16[4,512,2,128]{3,1,2,0:T(8,128)(2,1)}) %all-gather.5.cloned.1.call-update) | async-done | bytes 1048592 | tf_op jit(solution)/shard_map/all_gather | solution.py:68
  53.3 6.1 %conditional.8 = (f32[128,2,6]{0,2,1:T(8,128)}, f32[128,2,6]{0,2,1:T(8,128)S(1)}, f32[128,2,6,128]{3,0,2,1:T(8,128)S(1)}) conditional(s32[]{:T(128)} %convert_element_type.66, () %tuple.87, (bf16[4,512,2,128]{3,1,2,0:T(8,128)(2,1)}, bf16[2,128,2,6,128]{4,1,3,2,0:T(8,128)(2,1)}, bf16[4,512,2,128]{3,1,2,0:T(8,128)(2,1)}) %tuple.198), branch_computations={%region_0.0_spmd, %region_1.0_spmd} | conditional | flops 409147392 | bytes 11210776 | solution.py:81
  53.3 1.7 bitcast_reduce_fusion
  55.0 0.6 exponential_multiply_fusion
  55.6 1.2 fusion.2
  56.8 0.7 fusion.21
  57.5 1.9 fusion.10
  59.4 6.1 %conditional.12 = (f32[128,2,6]{0,2,1:T(8,128)}, f32[128,2,6]{0,2,1:T(8,128)S(1)}, f32[128,2,6,128]{3,0,2,1:T(8,128)S(1)}) conditional(s32[]{:T(128)} %convert_element_type.70, () %tuple.93, (bf16[4,512,2,128]{3,1,2,0:T(8,128)(2,1)}, bf16[2,128,2,6,128]{4,1,3,2,0:T(8,128)(2,1)}, bf16[4,512,2,128]{3,1,2,0:T(8,128)(2,1)}) %tuple.201), branch_computations={%region_16.0_spmd, %region_17.0_spmd} | conditional | flops 409147392 | bytes 11210776 | solution.py:81
  59.4 1.7 bitcast_reduce_fusion.4
  61.1 0.6 exponential_multiply_fusion.1
  61.7 1.2 fusion.85
  62.9 0.7 fusion.104
  63.6 1.9 fusion.93
  65.5 6.2 %conditional.13 = ((f32[128,2,6]{0,2,1:T(8,128)}, f32[128,2,6]{0,2,1:T(8,128)S(1)}, f32[128,2,6,128]{3,0,2,1:T(8,128)S(1)})) conditional(s32[]{:T(128)} %convert_element_type.69, (f32[128,2,6]{0,2,1:T(8,128)}, f32[128,2,6]{0,2,1:T(8,128)S(1)}, f32[128,2,6,128]{3,0,2,1:T(8,128)S(1)}) %conditional.12, (f32[128,2,6]{0,2,1:T(8,128)}, ...), branch_computations={%region_20.0_spmd, %region_21.0_spmd} | conditional | flops 409344000 | bytes 12032032 | solution.py:81
  65.5 1.7 bitcast_reduce_fusion.5
  67.2 0.7 multiply_add_fusion.5
  68.4 0.7 multiply_add_fusion.4
  69.1 2.0 fusion.115
  71.8 1.5 conditional.11
  72.0 1.2 copy.128
  73.8 0.9 copy-done.5
  74.8 1.6 copy.96
  76.4 2.0 fusion.174
  78.4 1.8 collective-permute-start
  80.2 2.1 collective-permute-start.1
  82.3 3.7 %fusion.172 = bf16[2,128,1536]{2,1,0:T(8,128)(2,1)S(1)} fusion(bf16[2,128,1536]{2,1,0:T(8,128)(2,1)S(1)} %fusion.174, bf16[1536,1536]{1,0:T(8,128)(2,1)} %param.25), kind=kOutput, calls=%fused_computation.170 | convolution fusion | flops 1207959552 | bytes 6291456 | tf_op jit(solution)/shard_map/ctf,fo->cto/dot_general | solution.py:96
  86.0 1.6 broadcast_in_dim.2
  87.6 0.9 copy_dynamic-update-slice_fusion.3
  88.5 3.8 %collective-permute-done = bf16[2,128,1536]{2,1,0:T(8,128)(2,1)S(1)} collective-permute-done((bf16[2,128,1536]{2,1,0:T(8,128)(2,1)S(1)}, bf16[2,128,1536]{2,1,0:T(8,128)(2,1)S(1)}, u32[]{:S(2)}, u32[]{:S(2)}) %collective-permute-start) | collective-permute-done | bytes 786464 | tf_op jit(solution)/shard_map/ppermute | solution.py:11
  92.4 1.4 fusion.170
  93.7 0.9 copy_dynamic-update-slice_fusion.2
  94.6 6.0 %collective-permute-done.1 = bf16[2,128,1536]{2,1,0:T(8,128)(2,1)S(1)} collective-permute-done((bf16[2,128,1536]{2,1,0:T(8,128)(2,1)S(1)}, bf16[2,128,1536]{2,1,0:T(8,128)(2,1)S(1)}, u32[]{:S(2)}, u32[]{:S(2)}) %collective-permute-start.1) | collective-permute-done | bytes 786464 | tf_op jit(solution)/shard_map/ppermute | solution.py:11
  100.6 1.4 fusion.168
  102.0 0.9 copy_dynamic-update-slice_fusion.1
  102.9 6.2 %collective-permute-done.2 = bf16[2,128,1536]{2,1,0:T(8,128)(2,1)S(1)} collective-permute-done((bf16[2,128,1536]{2,1,0:T(8,128)(2,1)S(1)}, bf16[2,128,1536]{2,1,0:T(8,128)(2,1)S(1)}, u32[]{:S(2)}, u32[]{:S(2)}) %collective-permute-start.2) | collective-permute-done | bytes 786464 | tf_op jit(solution)/shard_map/ppermute | solution.py:26
  109.1 1.4 fusion.166
  110.5 0.9 copy_dynamic-update-slice_fusion
  111.4 58.1 %all_to_all.18 = bf16[2,512,1536]{2,0,1:T(2,128)(2,1)S(1)} all-to-all(bf16[2,512,1536]{2,0,1:T(2,128)(2,1)S(1)} %copy_dynamic-update-slice_fusion), channel_id=1, replica_groups=mesh['rep'=2,'span'=2,'seq'=4,'tp'=2] {'seq'}, dimensions={1} | all-to-all | bytes 6291456 | tf_op jit(solution)/shard_map/all_to_all | solution.py:101
  169.5 2.2 copy.101
  171.7 4.6 %copy.102 = bf16[2,128,4,1536]{1,3,2,0:T(8,128)(2,1)} copy(bf16[2,128,4,1536]{3,1,2,0:T(8,128)(2,1)} %bitcast.335) | data formatting | bytes 6291456 | tf_op jit(solution)/shard_map/all_to_all | solution.py:101
  176.3 0.6 copy-done.7
  177.4 75.5 %reduce-scatter.2.cloned.1.call-done = bf16[2,128,3072]{1,2,0:T(8,128)(2,1)} async-done(((bf16[2,128,6144]{1,2,0:T(8,128)(2,1)}), bf16[2,128,3072]{1,2,0:T(8,128)(2,1)}) %reduce-scatter.2.cloned.1.call-update) | async-done | bytes 1572880 | tf_op jit(solution)/shard_map/reduce_scatter | solution.py:104
  252.9 2.1 multiply_convert_fusion
  255.0 1.6 copy.103
  (32 shorter events, 3.2 us)
Async XLA Ops:
  6.5 170.5 %copy-start = (f32[64,3072]{1,0:T(8,128)S(1)}, f32[64,3072]{1,0:T(8,128)}, u32[]{:S(2)}) copy-start(f32[64,3072]{1,0:T(8,128)} %param.26) | copy-start | bytes 2359300
  6.5 37.2 %all-gather.3.cloned.1.call-start = ((), (), s32[]{:S(2)}) async-start(), calls=%async_computation.2 | async-start | bytes 1572864 | tf_op jit(solution)/shard_map/all_gather | solution.py:67
  25.6 27.7 %all-gather.5.cloned.1.call-start = ((), (), s32[]{:S(2)}) async-start(), calls=%async_computation.3 | async-start | bytes 1572864 | tf_op jit(solution)/shard_map/all_gather | solution.py:68
  43.6 209.3 %reduce-scatter.2.cloned.1.call-start = ((), (), s32[]{:S(2)}) async-start(), calls=%async_computation.4 | async-start | bytes 4718592 | tf_op jit(solution)/shard_map/reduce_scatter | solution.py:104
  73.8 0.9 copy-start.5
  74.7 1.7 copy-start.6
  76.4 16.0 %slice-start = ((s8[4718592]{0:T(1024)(128)(4,1)}), s8[4194304]{0:T(1024)(128)(4,1)S(1)}, s32[]{:S(2)}) async-start(s8[4718592]{0:T(1024)(128)(4,1)} %bitcast.343), calls=%async_computation.5 | async-start | bytes 8388608
  78.4 14.0 %slice-start.1 = ((s8[4718592]{0:T(1024)(128)(4,1)}), s8[524288]{0:T(1024)(128)(4,1)S(1)}, s32[]{:S(2)}) async-start(s8[4718592]{0:T(1024)(128)(4,1)} %bitcast.343), calls=%async_computation.6 | async-start | bytes 1048576
  78.4 13.9 %collective-permute-start = (bf16[2,128,1536]{2,1,0:T(8,128)(2,1)S(1)}, bf16[2,128,1536]{2,1,0:T(8,128)(2,1)S(1)}, u32[]{:S(2)}, u32[]{:S(2)}) collective-permute-start(bf16[2,128,1536]{2,1,0:T(8,128)(2,1)S(1)} %fusion.174), channel_id=1, source_target_pairs={{0,2},{2,4},{4,6},{6,0},{1,3},{3,5},{5,7},{7,1},{8,10},{10,12},{12... | collective-permute-start | bytes 2359304 | tf_op jit(solution)/shard_map/ppermute | solution.py:11
  80.2 20.4 %collective-permute-start.1 = (bf16[2,128,1536]{2,1,0:T(8,128)(2,1)S(1)}, bf16[2,128,1536]{2,1,0:T(8,128)(2,1)S(1)}, u32[]{:S(2)}, u32[]{:S(2)}) collective-permute-start(bf16[2,128,1536]{2,1,0:T(8,128)(2,1)S(1)} %fusion.174), channel_id=1, source_target_pairs={{2,0},{4,2},{6,4},{0,6},{3,1},{5,3},{7,5},{1,7},{10,8},{12,10},{14... | collective-permute-start | bytes 2359304 | tf_op jit(solution)/shard_map/ppermute | solution.py:11
  92.3 16.8 %collective-permute-start.2 = (bf16[2,128,1536]{2,1,0:T(8,128)(2,1)S(1)}, bf16[2,128,1536]{2,1,0:T(8,128)(2,1)S(1)}, u32[]{:S(2)}, u32[]{:S(2)}) collective-permute-start(bf16[2,128,1536]{2,1,0:T(8,128)(2,1)S(1)} %collective-permute-done), channel_id=1, source_target_pairs={{0,2},{2,4},{4,6},{6,0},{1,3},{3,5},{5,7},{7,1},{8,10},{10,12},{12... | collective-permute-start | bytes 2359304 | tf_op jit(solution)/shard_map/ppermute | solution.py:26
  176.3 0.7 copy-start.7
Sparse Core Ops, SparseCore 0:
  25.7 10.8 all-gather.2
  43.7 9.5 all-gather.4
  176.5 76.3 reduce-scatter.1
